TPU v7x, 32 devices: a whole 2x2x4 slice. The times are simulated.
32 devices in a mesh: parts: 2 (over y), leaf: 4 (over z), mid: 2 (over x), top: 2 (over core).
Axes of the slice: x: 2, y: 2, z: 4, core: 2. Of those that a mesh axis runs over, the one named last changes fastest.
Arguments:
- leaf_precision: float32 [8, 2, 2, 128, 128], P(('parts', 'leaf'), 'mid', 'top'), parts along dimension 0, may hold values from -40 to 40, as said below
- basis_fine: float32 [8, 2, 2, 128, 128], P(('parts', 'leaf'), 'mid', 'top'), parts along dimension 0, may hold values from -1 to 1
- basis_mid: float32 [8, 2, 2, 128, 128], P(('parts', 'leaf'), 'mid', 'top'), parts along dimension 0, may hold values from -1 to 1
- basis_coarse: float32 [8, 2, 2, 128, 128], P(('parts', 'leaf'), 'mid', 'top'), parts along dimension 0, may hold values from -1 to 1
- core_fine: float32 [128, 128], replicated, may hold values from -20 to 20, as said below
- core_mid: float32 [128, 128], replicated, may hold values from -20 to 20, as said below
- core_coarse: float32 [128, 128], replicated, may hold values from -20 to 20, as said below
- observations: float32 [8, 2, 2, 128, 128], P(('parts', 'leaf'), 'mid', 'top'), parts along dimension 0, may hold values from -20 to 20
Outputs:
- solution: float32 [8, 2, 2, 128, 128], P(('parts', 'leaf'), 'mid', 'top'), parts along dimension 0
There are 2 independent parts, one for each index of `parts`. A program takes and returns all parts, laid end to end along the dimension named above; an argument that names none is the same for every part. Nothing has to cross between parts.
Inputs may be any that keep to these rules, and one draw needn't show every extreme that they name: Every leaf_precision[l, m, t] is symmetric positive definite. `core_fine`: symmetric positive definite. `core_mid`: symmetric positive definite. `core_coarse`: symmetric positive definite.
All inputs are finite; a program needn't handle non-finite values.
Results may differ from a plain program's by a relative error of at most 0.00005.
Values sent between devices are 32-bit elements; how exact they have to be, the bound alone decides.
A program may use at most 64 MiB of HBM per device.

v0:
```python
import functools

import jax
import jax.numpy as jnp
from jax import lax
from jax.experimental import pallas as pl
from jax.experimental.pallas import tpu as pltpu
from jax.sharding import PartitionSpec as P

MESH = pl.DeviceIdType.MESH
PANEL = 8


def dot(left_hand, right_side):
    return jnp.dot(
        left_hand, right_side, precision=lax.Precision.HIGHEST, preferred_element_type=jnp.float32
    )


def split3(x):
    high = x.astype(jnp.bfloat16).astype(jnp.float32)
    rest = x - high
    mid = rest.astype(jnp.bfloat16).astype(jnp.float32)
    low = (rest - mid).astype(jnp.bfloat16).astype(jnp.float32)
    return high, mid, low


def spread_panel(panel):
    p1, p2, p3 = split3(panel)
    return jnp.concatenate([p1, p1, p2, p2, p1, p3], axis=0).T.astype(jnp.bfloat16)


def rank_update(spread, scaled):
    r1, r2, r3 = split3(scaled)
    right_side = jnp.concatenate([r1, r2, r1, r2, r3, r1], axis=0).astype(jnp.bfloat16)
    return jnp.dot(spread, right_side, preferred_element_type=jnp.float32)


def negated_inverse(a_ref, matrix):
    size = matrix.shape[0]
    zero = jnp.zeros((PANEL, size), jnp.float32)
    a_ref[pl.ds(0, PANEL), :] = zero
    a_ref[pl.ds(PANEL, size), :] = matrix
    a_ref[pl.ds(PANEL + size, PANEL), :] = zero
    lane = lax.broadcasted_iota(jnp.int32, (PANEL, size), 1)
    sub = lax.broadcasted_iota(jnp.int32, (PANEL, size), 0)
    lane_full = lax.broadcasted_iota(jnp.int32, (size, size), 1)

    def columns(block, k):
        return [
            jnp.broadcast_to(
                jnp.sum(jnp.where(lane == k * PANEL + j, block, 0.0), axis=1, keepdims=True),
                block.shape,
            )
            for j in range(PANEL)
        ]

    def apply(k, spread, scaled):
        inside = (lane_full >= k * PANEL) & (lane_full < (k + 1) * PANEL)
        current = a_ref[pl.ds(PANEL, size), :]
        a_ref[pl.ds(PANEL, size), :] = jnp.where(inside, 0.0, current) - rank_update(spread, scaled)
        a_ref[pl.ds(pl.multiple_of((k + 1) * PANEL, PANEL), PANEL), :] = scaled

    def body(k, carry):
        spread_before, scaled_before, panel = carry
        apply(k - 1, spread_before, scaled_before)
        spread = spread_panel(panel)
        inside = (lane >= k * PANEL) & (lane < (k + 1) * PANEL)
        cols = columns(panel, k)
        ahead = lane == (k + 1) * PANEL + sub
        coefs = [
            jnp.broadcast_to(
                jnp.sum(
                    jnp.where(ahead, jnp.broadcast_to(panel[j : j + 1], panel.shape), 0.0),
                    axis=1, keepdims=True,
                ),
                panel.shape,
            )
            for j in range(PANEL)
        ]
        x = jnp.where(inside, jnp.where(lane - k * PANEL == sub, 1.0, 0.0), panel)
        for i in range(PANEL):
            pivot = 1.0 / jnp.broadcast_to(cols[i][i : i + 1], x.shape)
            here = sub == i

            def step(v):
                row = jnp.broadcast_to(v[i : i + 1], v.shape) * pivot
                return jnp.where(here, row, v - cols[i] * row)

            x_new = step(x)
            for j in range(i + 1, PANEL):
                cols[j] = step(cols[j])
            x = x_new
        scaled = jnp.where(inside, -x, x)
        following = a_ref[pl.ds(pl.multiple_of((k + 2) * PANEL, PANEL), PANEL), :]
        panel_next = jnp.where(inside, 0.0, following)
        for j in range(PANEL):
            panel_next = panel_next - coefs[j] * jnp.broadcast_to(scaled[j : j + 1], x.shape)
        return spread, scaled, panel_next

    steps = size // PANEL
    spread, scaled, _ = lax.fori_loop(0, steps, body, (spread_panel(zero), zero, matrix[:PANEL]))
    apply(steps - 1, spread, scaled)
    return a_ref[pl.ds(PANEL, size), :]


def kernel(
    n_leaf, n_mid, n_top,
    prec_ref, fine_ref, mid_ref, coarse_ref, core_fine_ref, core_mid_ref, core_coarse_ref, obs_ref,
    out_ref,
    a_ref, bulk_ref, rs_in, pair_in, cross_ref, cross_in, part_ref, ag_ref, piece_ref, piece_in, quarter_ref, s_ref, top_ref, top_in,
    rs_send, rs_recv, pair_send, pair_recv, cross_send, cross_recv, ag_send, ag_recv, mid_send, mid_recv, s_send, s_recv, top_send, top_recv,
):
    r = fine_ref.shape[1]
    rows = r // n_leaf
    leaf, mid, top = lax.axis_index("leaf"), lax.axis_index("mid"), lax.axis_index("top")
    own_rows = pl.ds(pl.multiple_of(leaf * rows, rows), rows)
    barrier = pltpu.get_barrier_semaphore()
    places = {"leaf": (leaf, n_leaf), "mid": (mid, n_mid), "top": (top, n_top)}

    far_first = sorted(range(1, n_leaf), key=lambda step: (abs(2 * step - n_leaf), step))

    def peer(axis, step):
        index, count = places[axis]
        return {axis: lax.rem(index + step, count)}

    for axis in places:
        for step in range(1, places[axis][1]):
            pl.semaphore_signal(barrier, inc=1, device_id=peer(axis, step), device_id_type=MESH)

    def send(src, dst, sems, phase, axis, step):
        copy = pltpu.make_async_remote_copy(
            src_ref=src, dst_ref=dst,
            send_sem=sems[0].at[phase, step - 1], recv_sem=sems[1].at[phase, step - 1],
            device_id=peer(axis, step), device_id_type=MESH,
        )
        copy.start()
        return copy

    def span(blocks):
        return slice(blocks[0] * r, blocks[1] * r)

    def scatter(phase, blocks):
        copies = {}
        for step in far_first:
            target = lax.rem(leaf + step, n_leaf)
            target_rows = pl.ds(pl.multiple_of(target * rows, rows), rows)
            copies[step] = send(
                bulk_ref.at[target_rows, span(blocks)], rs_in.at[step - 1, :, span(blocks)],
                (rs_send, rs_recv), phase, "leaf", step,
            )
        return copies, blocks

    def collect(handle):
        copies, blocks = handle
        total = bulk_ref[own_rows, span(blocks)]
        for step in range(1, n_leaf):
            copies[step].wait()
            total = total + rs_in[step - 1, :, span(blocks)]
        return total

    half = n_leaf // 2
    parity = lax.rem(leaf, 2)

    def row_block(index):
        return pl.ds(pl.multiple_of(index * rows, rows), rows)

    def shifted(blocks):
        return slice((blocks[0] - 4) * r, (blocks[1] - 4) * r)

    def pair_scatter(phase, blocks):
        copies = []
        for j in range(half):
            copy = pltpu.make_async_remote_copy(
                src_ref=bulk_ref.at[row_block(2 * j + 1 - parity), span(blocks)],
                dst_ref=pair_in.at[j, :, shifted(blocks)],
                send_sem=pair_send.at[phase, j], recv_sem=pair_recv.at[phase, j],
                device_id={"leaf": leaf + 1 - 2 * parity}, device_id_type=MESH,
            )
            copy.start()
            copies.append(copy)
        return copies

    def cross_scatter(phase, blocks, pair_copies):
        for copy in pair_copies:
            copy.wait()
        columns = shifted(blocks)
        copies = []
        for step in range(1, half):
            target = lax.rem(leaf + 2 * step, n_leaf)
            cross_ref[step - 1, :, columns] = (
                bulk_ref[row_block(target), span(blocks)]
                + pair_in[lax.div(target, 2), :, columns]
            )
            copy = pltpu.make_async_remote_copy(
                src_ref=cross_ref.at[step - 1, :, columns],
                dst_ref=cross_in.at[step - 1, :, columns],
                send_sem=cross_send.at[phase, step - 1], recv_sem=cross_recv.at[phase, step - 1],
                device_id={"leaf": target}, device_id_type=MESH,
            )
            copy.start()
            copies.append(copy)
        return copies, blocks

    def cross_collect(handle):
        copies, blocks = handle
        columns = shifted(blocks)
        total = bulk_ref[own_rows, span(blocks)] + pair_in[lax.div(leaf, 2), :, columns]
        for step, copy in enumerate(copies):
            copy.wait()
            total = total + cross_in[step, :, columns]
        return total

    def gather(source, target, sems, phase, blocks, value):
        source[:, span(blocks)] = value
        copies = [
            send(
                source.at[:, span(blocks)], target.at[own_rows, span(blocks)],
                sems, phase, "leaf", step,
            )
            for step in far_first
        ]
        target[own_rows, span(blocks)] = value
        return copies

    def exchange(axis, source, target, sems, phase, blocks, value):
        source[:, span(blocks)] = value
        copies = [
            send(
                source.at[:, span(blocks)], target.at[step - 1, :, span(blocks)],
                sems, phase, axis, step,
            )
            for step in range(1, places[axis][1])
        ]
        return copies, target, blocks, value

    def add_up(handle):
        copies, target, blocks, total = handle
        for step, copy in enumerate(copies):
            copy.wait()
            total = total + target[step, :, span(blocks)]
        return total

    def wait_all(copies):
        for copy in copies:
            copy.wait()

    def put(place, value):
        bulk_ref[:, place * r : (place + 1) * r] = value

    prec = prec_ref[...]
    fine, middle, coarse = fine_ref[...], mid_ref[...], coarse_ref[...]
    solved_f = dot(prec, fine)
    fine_t = fine.T
    put(0, dot(fine_t, solved_f))
    pl.semaphore_wait(barrier, (n_leaf - 1) + (n_mid - 1) + (n_top - 1))
    rs_ff = scatter(0, (0, 1))
    mid_t, coarse_t = middle.T, coarse.T
    solved_y = dot(prec, obs_ref[...])
    put(1, dot(mid_t, solved_f))
    put(2, dot(coarse_t, solved_f))
    put(3, dot(fine_t, solved_y))
    rs_f = scatter(1, (1, 4))
    solved_m, solved_c = dot(prec, middle), dot(prec, coarse)
    put(4, dot(mid_t, solved_m))
    put(5, dot(mid_t, solved_c))
    put(6, dot(mid_t, solved_y))
    put(7, dot(coarse_t, solved_c))
    put(8, dot(coarse_t, solved_y))

    first = (ag_send, ag_recv)
    ag_ff = gather(part_ref, ag_ref, first, 0, (0, 1), collect(rs_ff))
    pair_m = pair_scatter(0, (4, 7))
    part_f = collect(rs_f)
    ag_f = gather(part_ref, ag_ref, first, 1, (1, 4), part_f)
    pair_c = pair_scatter(1, (7, 9))
    rs_m = cross_scatter(0, (4, 7), pair_m)

    wait_all(ag_ff)
    fine_inverse = negated_inverse(a_ref, core_fine_ref[...] + ag_ref[:, :r])
    rs_c = cross_scatter(1, (7, 9), pair_c)
    wait_all(ag_f)
    q_m, q_c = part_f[:, :r], part_f[:, r : 2 * r]
    w_m = dot(fine_inverse, ag_ref[:, r : 2 * r].T)
    part_m = cross_collect(rs_m)
    between, second = (mid_send, mid_recv), (s_send, s_recv)
    x_mm = exchange("mid", piece_ref, piece_in, between, 0, (0, 1), part_m[:, :r] + dot(q_m, w_m))
    w_c = dot(fine_inverse, ag_ref[:, 2 * r : 3 * r].T)
    w_y = dot(fine_inverse, ag_ref[:, 3 * r : 4 * r])
    cross_piece = jnp.concatenate(
        [part_m[:, r : 2 * r] + dot(q_m, w_c), part_m[:, 2 * r :] + dot(q_m, w_y)], axis=1
    )
    x_mc = exchange("mid", piece_ref, piece_in, between, 1, (1, 3), cross_piece)
    ag_mm = gather(quarter_ref, s_ref, second, 0, (0, 1), add_up(x_mm))
    ag_mc = gather(quarter_ref, s_ref, second, 1, (1, 3), add_up(x_mc))
    part_c = cross_collect(rs_c)
    coarse_piece = jnp.concatenate(
        [part_c[:, :r] + dot(q_c, w_c), part_c[:, r:] + dot(q_c, w_y)], axis=1
    )
    x_cc = exchange("mid", piece_ref, piece_in, between, 2, (3, 5), coarse_piece)
    coarse_sum = add_up(x_cc)
    ag_cc = gather(quarter_ref, s_ref, second, 2, (3, 4), coarse_sum[:, :r])
    ag_cy = gather(quarter_ref, s_ref, second, 3, (4, 5), coarse_sum[:, r:])

    wait_all(ag_mm)
    mid_inverse = negated_inverse(a_ref, core_mid_ref[...] + s_ref[:, :r])
    wait_all(ag_mc)
    cross = s_ref[:, r : 2 * r]
    cross_t = cross.T
    v_c = dot(mid_inverse, cross)
    last = (top_send, top_recv)
    cross_cc = dot(cross_t, v_c)
    wait_all(ag_cc)
    x_top = exchange("top", top_ref, top_in, last, 0, (0, 1), s_ref[:, 3 * r : 4 * r] + cross_cc)
    v_y = dot(mid_inverse, s_ref[:, 2 * r : 3 * r])
    cross_cy = dot(cross_t, v_y)
    wait_all(ag_cy)
    x_right = exchange("top", top_ref, top_in, last, 1, (1, 2), s_ref[:, 4 * r : 5 * r] + cross_cy)
    coarse_inverse = negated_inverse(a_ref, core_coarse_ref[...] + add_up(x_top))
    x_c = -dot(coarse_inverse, add_up(x_right))
    x_m = dot(v_c, x_c) - v_y
    x_f = dot(w_m, x_m) + dot(w_c, x_c) - w_y
    out_ref[...] = solved_y - dot(solved_f, x_f) - dot(solved_m, x_m) - dot(solved_c, x_c)


def local(n_leaf, n_mid, n_top, *operands):
    blocks = [x.reshape(x.shape[-2:]) for x in operands]
    r = blocks[1].shape[1]
    rows = r // n_leaf
    half = n_leaf // 2
    f32 = jnp.float32

    def pair(phases, count):
        return [pltpu.SemaphoreType.DMA((phases, count - 1))] * 2

    answer = pl.pallas_call(
        functools.partial(kernel, n_leaf, n_mid, n_top),
        out_shape=jax.ShapeDtypeStruct(blocks[-1].shape, f32),
        in_specs=[pl.BlockSpec(memory_space=pltpu.VMEM)] * len(blocks),
        out_specs=pl.BlockSpec(memory_space=pltpu.VMEM),
        scratch_shapes=[
            pltpu.VMEM((r + 2 * PANEL, r), f32),
            pltpu.VMEM((r, 9 * r), f32),
            pltpu.VMEM((n_leaf - 1, rows, 4 * r), f32),
            pltpu.VMEM((half, rows, 5 * r), f32),
            pltpu.VMEM((half - 1, rows, 5 * r), f32),
            pltpu.VMEM((half - 1, rows, 5 * r), f32),
            pltpu.VMEM((rows, 4 * r), f32),
            pltpu.VMEM((r, 4 * r), f32),
            pltpu.VMEM((rows, 5 * r), f32),
            pltpu.VMEM((n_mid - 1, rows, 5 * r), f32),
            pltpu.VMEM((rows, 5 * r), f32),
            pltpu.VMEM((r, 5 * r), f32),
            pltpu.VMEM((r, 2 * r), f32),
            pltpu.VMEM((n_top - 1, r, 2 * r), f32),
            *pair(2, n_leaf), *pair(2, half + 1), *pair(2, half), *pair(2, n_leaf), *pair(3, n_mid), *pair(4, n_leaf), *pair(2, n_top),
        ],
        compiler_params=pltpu.CompilerParams(collective_id=0, has_side_effects=True),
    )(*blocks)
    return answer[None, None, None]


def solution(mesh):
    spread = P(("parts", "leaf"), "mid", "top", None, None)
    sizes = (mesh.shape["leaf"], mesh.shape["mid"], mesh.shape["top"])
    return jax.shard_map(
        functools.partial(local, *sizes),
        mesh=mesh,
        in_specs=(spread, spread, spread, spread, P(), P(), P(), spread),
        out_specs=spread,
        check_vma=False,
    )
```

profile of v0, /device:TPU:0, one launch (start us, length us, event | category | flops | bytes accessed | tf_op | source)
XLA Modules:
  0.0 39.7 jit_solution(7861834367038829257)
XLA Ops:
  0.0 38.2 %shard_map.82 = f32[128,128]{1,0:T(8,128)} custom-call(f32[128,128]{1,0:T(8,128)} %bitcast.7, f32[128,128]{1,0:T(8,128)} %bitcast.8, f32[128,128]{1,0:T(8,128)} %bitcast.9, f32[128,128]{1,0:T(8,128)} %bitcast.10, f32[128,128]{1,0:T(8,128)} %core_fine_ref.1, f32[128,128]{1,0:T(8,128)} %core_mid_ref.1, f32[128,128]{1,0:T(8,128)} %core_coarse_ref.1, ...), custom_call_target="tpu_custom_call" | custom-call | tf_op jit(solution)/shard_map/pallas_call | solution.py:336
  38.2 1.5 %copy.10 = f32[1,1,1,128,128]{4,3,2,1,0:T(8,128)} copy(f32[1,1,1,128,128]{4,3,2,1,0:T(8,128)} %bitcast.6) | data formatting | bytes 131072
where the time goes:
time: 39.9 us; the launch traced here: 39.7 us
  Pallas kernels  38.2 us (96%)
  local copies, waits for them, and re-layouts  1.47 us (4%)
    pallas_call x1, Pallas kernels, local(): pl.pallas_call(functools.partial(kernel, n_leaf, n_mid, n_top), out_shape...  38.2 us
    unnamed x1, local copies, waits for them, and re-layouts  1.47 us

commit v1 on v0

v1 whole, which is shorter than its diff:
```python
import functools

import jax
import jax.numpy as jnp
from jax import lax
from jax.experimental import pallas as pl
from jax.experimental.pallas import tpu as pltpu
from jax.sharding import PartitionSpec as P

MESH = pl.DeviceIdType.MESH
PANEL = 8


def dot(left_hand, right_side):
    return jnp.dot(
        left_hand, right_side, precision=lax.Precision.HIGHEST, preferred_element_type=jnp.float32
    )


def split3(x):
    high = x.astype(jnp.bfloat16).astype(jnp.float32)
    rest = x - high
    mid = rest.astype(jnp.bfloat16).astype(jnp.float32)
    low = (rest - mid).astype(jnp.bfloat16).astype(jnp.float32)
    return high, mid, low


def spread_panel(panel):
    p1, p2, p3 = split3(panel)
    return jnp.concatenate([p1, p1, p2, p2, p1, p3], axis=0).T.astype(jnp.bfloat16)


def rank_update(spread, scaled):
    r1, r2, r3 = split3(scaled)
    right_side = jnp.concatenate([r1, r2, r1, r2, r3, r1], axis=0).astype(jnp.bfloat16)
    return jnp.dot(spread, right_side, preferred_element_type=jnp.float32)


def negated_inverse(a_ref, matrix):
    size = matrix.shape[0]
    zero = jnp.zeros((PANEL, size), jnp.float32)
    a_ref[pl.ds(0, PANEL), :] = zero
    a_ref[pl.ds(PANEL, size), :] = matrix
    a_ref[pl.ds(PANEL + size, PANEL), :] = zero
    lane = lax.broadcasted_iota(jnp.int32, (PANEL, size), 1)
    sub = lax.broadcasted_iota(jnp.int32, (PANEL, size), 0)
    lane_full = lax.broadcasted_iota(jnp.int32, (size, size), 1)

    def columns(block, k):
        return [
            jnp.broadcast_to(
                jnp.sum(jnp.where(lane == k * PANEL + j, block, 0.0), axis=1, keepdims=True),
                block.shape,
            )
            for j in range(PANEL)
        ]

    def apply(k, spread, scaled):
        inside = (lane_full >= k * PANEL) & (lane_full < (k + 1) * PANEL)
        current = a_ref[pl.ds(PANEL, size), :]
        a_ref[pl.ds(PANEL, size), :] = jnp.where(inside, 0.0, current) - rank_update(spread, scaled)
        a_ref[pl.ds(pl.multiple_of((k + 1) * PANEL, PANEL), PANEL), :] = scaled

    def body(k, carry):
        spread_before, scaled_before, panel = carry
        apply(k - 1, spread_before, scaled_before)
        spread = spread_panel(panel)
        inside = (lane >= k * PANEL) & (lane < (k + 1) * PANEL)
        cols = columns(panel, k)
        ahead = lane == (k + 1) * PANEL + sub
        coefs = [
            jnp.broadcast_to(
                jnp.sum(
                    jnp.where(ahead, jnp.broadcast_to(panel[j : j + 1], panel.shape), 0.0),
                    axis=1, keepdims=True,
                ),
                panel.shape,
            )
            for j in range(PANEL)
        ]
        x = jnp.where(inside, jnp.where(lane - k * PANEL == sub, 1.0, 0.0), panel)
        for i in range(PANEL):
            pivot = 1.0 / jnp.broadcast_to(cols[i][i : i + 1], x.shape)
            here = sub == i

            def step(v):
                row = jnp.broadcast_to(v[i : i + 1], v.shape) * pivot
                return jnp.where(here, row, v - cols[i] * row)

            x_new = step(x)
            for j in range(i + 1, PANEL):
                cols[j] = step(cols[j])
            x = x_new
        scaled = jnp.where(inside, -x, x)
        following = a_ref[pl.ds(pl.multiple_of((k + 2) * PANEL, PANEL), PANEL), :]
        panel_next = jnp.where(inside, 0.0, following)
        for j in range(PANEL):
            panel_next = panel_next - coefs[j] * jnp.broadcast_to(scaled[j : j + 1], x.shape)
        return spread, scaled, panel_next

    steps = size // PANEL
    spread, scaled, _ = lax.fori_loop(0, steps, body, (spread_panel(zero), zero, matrix[:PANEL]))
    apply(steps - 1, spread, scaled)
    return a_ref[pl.ds(PANEL, size), :]


def dot_nt(left_hand, right_rows):
    return lax.dot_general(
        left_hand, right_rows, (((1,), (1,)), ((), ())),
        precision=lax.Precision.HIGHEST, preferred_element_type=jnp.float32,
    )


def pack(matrix):
    half, size = matrix.shape[0] // 2, matrix.shape[1]
    lane = lax.broadcasted_iota(jnp.int32, (half, size), 1)
    row = lax.broadcasted_iota(jnp.int32, (half, size), 0)
    bottom = pltpu.roll(matrix[half:], half, 1)
    main = jnp.where(lane < row, bottom, matrix[:half])
    diagonal = jnp.sum(jnp.where(lane == row, bottom, 0.0), axis=0, keepdims=True)
    return main, jnp.broadcast_to(diagonal, (PANEL, size))


def unpack(main, diagonal):
    half, size = main.shape
    lane = lax.broadcasted_iota(jnp.int32, (half, size), 1)
    row = lax.broadcasted_iota(jnp.int32, (half, size), 0)
    flipped = jnp.concatenate([main, main], axis=0).T
    top = jnp.where(lane < row, flipped[:half], main)
    lower = jnp.where(lane < row, main, flipped[:half])
    lower = jnp.where(lane == row, jnp.broadcast_to(diagonal[:1], lower.shape), lower)
    bottom = jnp.where(lane < half, flipped[half:], pltpu.roll(lower, half, 1))
    return jnp.concatenate([top, bottom], axis=0)


FF, MF, MM, CF, CM, CC, YF, YM, YC = range(9)
SYMMETRIC = (FF, MM, CC)


def kernel(
    n_leaf, n_mid, n_top,
    prec_hbm, fine_hbm, mid_hbm, coarse_hbm, core_fine_hbm, core_mid_hbm, core_coarse_hbm, obs_hbm,
    out_ref,
    in_ref, a_ref, s_ref, bulk_ref, gram_in, pass_ref, total_ref, fine_ref, mid_ref, cross_ref, cross_in, last_ref,
    in_sem, gram_send, gram_recv, fine_send, fine_recv, mid_send, mid_recv, cross_send, cross_recv, last_send, last_recv,
):
    r = bulk_ref.shape[1]
    packed = r // 2 + PANEL
    leaf, mid, top = lax.axis_index("leaf"), lax.axis_index("mid"), lax.axis_index("top")

    def root_of(index):
        return (n_leaf - 1) // 2 + lax.rem(index, 2) * (n_leaf // 2 - (n_leaf - 1) // 2)

    root = root_of(top)
    is_root = leaf == root
    is_other = leaf != root
    barrier = pltpu.get_barrier_semaphore()

    def greet(device):
        pl.semaphore_signal(barrier, inc=1, device_id=device, device_id_type=MESH)

    leaf_steps = sorted(range(1, n_leaf), key=lambda step: (abs(2 * step - n_leaf), step))

    def along(axis, index, count, step):
        return {axis: lax.rem(index + step, count)}

    for t in range(n_top):
        @pl.when((leaf != root_of(t)) | (top != t))
        def _():
            greet({"leaf": root_of(t), "top": jnp.int32(t)})

    @pl.when(is_root)
    def _():
        for step in leaf_steps:
            greet(along("leaf", leaf, n_leaf, step))
        for step in range(1, n_mid):
            greet(along("mid", mid, n_mid, step))

    sources = [prec_hbm, fine_hbm, mid_hbm, coarse_hbm, obs_hbm, core_fine_hbm, core_mid_hbm, core_coarse_hbm]
    loads = [pltpu.make_async_copy(src, in_ref.at[k], in_sem.at[k]) for k, src in enumerate(sources)]
    for load in loads:
        load.start()

    def fetch(k):
        loads[k].wait()
        return in_ref[k]

    def rows(block):
        return slice(0, packed if block in SYMMETRIC else r)

    def gram_copy(block, slot):
        return pltpu.make_async_remote_copy(
            src_ref=bulk_ref.at[block, rows(block)], dst_ref=gram_in.at[slot, block, rows(block)],
            send_sem=gram_send.at[block], recv_sem=gram_recv.at[slot, block],
            device_id={"leaf": root}, device_id_type=MESH,
        )

    slot_here = lax.rem(root - leaf + n_leaf, n_leaf) - 1

    def store(ref, block, value, symmetric):
        if symmetric:
            main, diagonal = pack(value)
            ref[block, : r // 2] = main
            ref[block, r // 2 : packed] = diagonal
        else:
            ref[block] = value

    def hand_in(block, value):
        store(bulk_ref, block, value, block in SYMMETRIC)

        @pl.when(is_other)
        def _():
            gram_copy(block, slot_here).start()

    prec, fine = fetch(0), fetch(1)
    solved_f = dot(prec, fine)
    s_ref[0] = solved_f
    gram_ff = dot(fine.T, solved_f)

    @pl.when(is_root)
    def _():
        pl.semaphore_wait(barrier, n_leaf * n_top - 1 + n_mid - 1)

    @pl.when(is_other)
    def _():
        pl.semaphore_wait(barrier, 1)

    hand_in(FF, gram_ff)
    middle = fetch(2)
    mid_t = middle.T
    hand_in(MF, dot(mid_t, solved_f))
    solved_m = dot(prec, middle)
    s_ref[1] = solved_m
    hand_in(MM, dot(mid_t, solved_m))
    coarse = fetch(3)
    coarse_t = coarse.T
    hand_in(CF, dot(coarse_t, solved_f))
    hand_in(CM, dot(coarse_t, solved_m))
    solved_c = dot(prec, coarse)
    s_ref[2] = solved_c
    hand_in(CC, dot(coarse_t, solved_c))
    obs = fetch(4)
    obs_t = obs.T
    hand_in(YF, dot(obs_t, solved_f))
    hand_in(YM, dot(obs_t, solved_m))
    hand_in(YC, dot(obs_t, solved_c))
    s_ref[3] = dot(prec, obs)
    for k in range(5, 8):
        loads[k].wait()

    def spread(ref, sends, recvs, block, step):
        return pltpu.make_async_remote_copy(
            src_ref=ref.at[block], dst_ref=ref.at[block],
            send_sem=sends.at[block, step - 1], recv_sem=recvs.at[block],
            device_id=along("leaf", leaf, n_leaf, step), device_id_type=MESH,
        )

    def cross_copy(block, step):
        place = slice(0, packed if block in (0, 3) else r)
        return pltpu.make_async_remote_copy(
            src_ref=cross_ref.at[block, place], dst_ref=cross_in.at[step - 1, block, place],
            send_sem=cross_send.at[block, step - 1], recv_sem=cross_recv.at[block, step - 1],
            device_id=along("mid", mid, n_mid, step), device_id_type=MESH,
        )

    others = [(a, b) for a in [*leaf_steps, 0] for b in reversed(range(n_top)) if (a, b) != (0, 0)]

    def last_copy(block, source, number):
        a, b = others[number]
        place = slice(0, packed if block == 0 else r)
        return pltpu.make_async_remote_copy(
            src_ref=last_ref.at[source, block, place], dst_ref=last_ref.at[source, block, place],
            send_sem=last_send.at[block, number], recv_sem=last_recv.at[block, source],
            device_id={**along("leaf", leaf, n_leaf, a), **along("top", top, n_top, b)}, device_id_type=MESH,
        )

    def gathered(block):
        place = rows(block)
        total = bulk_ref[block, place]
        for slot in range(n_leaf - 1):
            gram_copy(block, slot).wait_recv()
            total = total + gram_in[slot, block, place]
        return total

    def whole(value):
        return unpack(value[: r // 2], value[r // 2 :])

    def cross_send_off(block, value, symmetric):
        store(cross_ref, block, value, symmetric)
        for step in range(1, n_mid):
            cross_copy(block, step).start()

    def crossed(block):
        place = slice(0, packed if block in (0, 3) else r)
        total = cross_ref[block, place]
        for step in range(1, n_mid):
            cross_copy(block, step).wait_recv()
            total = total + cross_in[step - 1, block, place]
        return total

    @pl.when(is_root)
    def _():
        inverse = negated_inverse(a_ref, in_ref[5] + whole(gathered(FF)))
        mf = gathered(MF)
        n_m = dot(mf, inverse)
        cross_send_off(0, whole(gathered(MM)) + dot_nt(n_m, mf), True)
        fine_ref[0] = n_m
        cf = gathered(CF)
        n_c = dot(cf, inverse)
        cross_send_off(1, gathered(CM) + dot_nt(n_c, mf), False)
        cross_send_off(3, whole(gathered(CC)) + dot_nt(n_c, cf), True)
        fine_ref[1] = n_c
        total_ref[0] = inverse
        total_ref[1] = mf
        total_ref[2] = cf
        for block in range(2):
            for step in leaf_steps:
                spread(fine_ref, fine_send, fine_recv, block, step).start()

        inverse = negated_inverse(a_ref, in_ref[6] + whole(crossed(0)))
        cm = crossed(1)
        q_c = dot(cm, inverse)
        store(last_ref.at[top], 0, whole(crossed(3)) + dot_nt(q_c, cm), True)
        for number in range(len(others)):
            last_copy(0, top, number).start()
        mid_ref[0] = q_c

        n_y = dot(gathered(YF), total_ref[0])
        cross_send_off(2, gathered(YM) + dot_nt(n_y, total_ref[1]), False)
        cross_send_off(4, gathered(YC) + dot_nt(n_y, total_ref[2]), False)
        fine_ref[2] = n_y
        for step in leaf_steps:
            spread(mid_ref, mid_send, mid_recv, 0, step).start()
            spread(fine_ref, fine_send, fine_recv, 2, step).start()
        q_y = dot(crossed(2), inverse)
        last_ref[top, 1] = crossed(4) + dot_nt(q_y, cm)
        for number in range(len(others)):
            last_copy(1, top, number).start()
        mid_ref[1] = q_y
        for step in leaf_steps:
            spread(mid_ref, mid_send, mid_recv, 1, step).start()

    def arrived(block):
        for t in range(n_top):
            @pl.when(is_other | (top != t))
            def _():
                last_copy(block, t, 0).wait_recv()

    arrived(0)
    coarse_sum = last_ref[0, 0, :packed]
    for t in range(1, n_top):
        coarse_sum = coarse_sum + last_ref[t, 0, :packed]
    inverse = negated_inverse(a_ref, in_ref[7] + whole(coarse_sum))

    @pl.when(is_other)
    def _():
        for block in range(3):
            spread(fine_ref, fine_send, fine_recv, block, 1).wait_recv()
        for block in range(2):
            spread(mid_ref, mid_send, mid_recv, block, 1).wait_recv()

    solved_f = s_ref[0]
    after_m = s_ref[1] + dot_nt(solved_f, fine_ref[0])
    after_c = s_ref[2] + dot_nt(solved_f, fine_ref[1]) + dot_nt(after_m, mid_ref[0])
    after_y = s_ref[3] + dot_nt(solved_f, fine_ref[2]) + dot_nt(after_m, mid_ref[1])
    arrived(1)
    right = last_ref[0, 1]
    for t in range(1, n_top):
        right = right + last_ref[t, 1]
    out_ref[...] = after_y + dot_nt(after_c, dot(right, inverse))

    @pl.when(is_root)
    def _():
        for block in range(5):
            for step in range(1, n_mid):
                cross_copy(block, step).wait_send()
        for step in leaf_steps:
            for block in range(3):
                spread(fine_ref, fine_send, fine_recv, block, step).wait_send()
            for block in range(2):
                spread(mid_ref, mid_send, mid_recv, block, step).wait_send()
        for block in range(2):
            for number in range(len(others)):
                last_copy(block, top, number).wait_send()

    @pl.when(is_other)
    def _():
        for block in range(9):
            gram_copy(block, slot_here).wait_send()


def local(n_leaf, n_mid, n_top, *operands):
    blocks = [x.reshape(x.shape[-2:]) for x in operands]
    r = blocks[1].shape[1]
    f32 = jnp.float32
    dma = pltpu.SemaphoreType.DMA
    answer = pl.pallas_call(
        functools.partial(kernel, n_leaf, n_mid, n_top),
        out_shape=jax.ShapeDtypeStruct(blocks[-1].shape, f32),
        in_specs=[pl.BlockSpec(memory_space=pl.ANY)] * len(blocks),
        out_specs=pl.BlockSpec(memory_space=pltpu.VMEM),
        scratch_shapes=[
            pltpu.VMEM((8, r, r), f32),
            pltpu.VMEM((r + 2 * PANEL, r), f32),
            pltpu.VMEM((4, r, r), f32),
            pltpu.VMEM((9, r, r), f32),
            pltpu.VMEM((n_leaf - 1, 9, r, r), f32),
            pltpu.VMEM((PANEL, r), f32),
            pltpu.VMEM((3, r, r), f32),
            pltpu.VMEM((3, r, r), f32),
            pltpu.VMEM((2, r, r), f32),
            pltpu.VMEM((5, r, r), f32),
            pltpu.VMEM((n_mid - 1, 5, r, r), f32),
            pltpu.VMEM((n_top, 2, r, r), f32),
            dma((8,)),
            dma((9,)), dma((n_leaf - 1, 9)),
            dma((3, n_leaf - 1)), dma((3,)),
            dma((2, n_leaf - 1)), dma((2,)),
            dma((5, n_mid - 1)), dma((5, n_mid - 1)),
            dma((2, n_leaf * n_top - 1)), dma((2, n_top)),
        ],
        compiler_params=pltpu.CompilerParams(collective_id=0, has_side_effects=True),
    )(*blocks)
    return answer[None, None, None]


def solution(mesh):
    spread = P(("parts", "leaf"), "mid", "top", None, None)
    sizes = (mesh.shape["leaf"], mesh.shape["mid"], mesh.shape["top"])
    return jax.shard_map(
        functools.partial(local, *sizes),
        mesh=mesh,
        in_specs=(spread, spread, spread, spread, P(), P(), P(), spread),
        out_specs=spread,
        check_vma=False,
    )
```

time: 39.9 us -> 34.2 us (0.86)
  Pallas kernels: 38.2 us -> 32.5 us
    pallas_call x1, Pallas kernels: 38.2 us -> 32.5 us  [local(): pl.pallas_call(functools.partial(kernel, n_leaf, n_mid, n_top), out_shape...]
where the time goes in v1:
time: 34.2 us; the launch traced here: 34 us
  Pallas kernels  32.5 us (95%)
  local copies, waits for them, and re-layouts  1.47 us (4%)
    pallas_call x1, Pallas kernels, local(): pl.pallas_call(functools.partial(kernel, n_leaf, n_mid, n_top), out_shape...  32.5 us
    unnamed x1, local copies, waits for them, and re-layouts  1.47 us

profile of v1, /device:TPU:0, one launch (start us, length us, event | category | flops | bytes accessed | tf_op | source)
XLA Modules:
  0.0 34.0 jit_solution(4867496327844174655)
XLA Ops:
  0.0 32.5 %shard_map.82 = f32[128,128]{1,0:T(8,128)} custom-call(f32[128,128]{1,0:T(8,128)} %bitcast.7, f32[128,128]{1,0:T(8,128)} %bitcast.8, f32[128,128]{1,0:T(8,128)} %bitcast.9, f32[128,128]{1,0:T(8,128)} %bitcast.10, f32[128,128]{1,0:T(8,128)} %core_fine_hbm.1, f32[128,128]{1,0:T(8,128)} %core_mid_hbm.1, f32[128,128]{1,0:T(8,128)} %core_coarse_hbm.1, ...), custom_call_target="tpu_custom_call" | custom-call | tf_op jit(solution)/shard_map/pallas_call | solution.py:397
  32.5 1.5 %copy.10 = f32[1,1,1,128,128]{4,3,2,1,0:T(8,128)} copy(f32[1,1,1,128,128]{4,3,2,1,0:T(8,128)} %bitcast.6) | data formatting | bytes 131072

commit v2 on v1

v2 whole, which is shorter than its diff:
```python
import functools

import jax
import jax.numpy as jnp
from jax import lax
from jax.experimental import pallas as pl
from jax.experimental.pallas import tpu as pltpu
from jax.sharding import PartitionSpec as P

MESH = pl.DeviceIdType.MESH
PANEL = 8


def dot(left_hand, right_side):
    return jnp.dot(
        left_hand, right_side, precision=lax.Precision.HIGHEST, preferred_element_type=jnp.float32
    )


def split3(x):
    high = x.astype(jnp.bfloat16).astype(jnp.float32)
    rest = x - high
    mid = rest.astype(jnp.bfloat16).astype(jnp.float32)
    low = (rest - mid).astype(jnp.bfloat16).astype(jnp.float32)
    return high, mid, low


def spread_panel(panel):
    p1, p2, p3 = split3(panel)
    return jnp.concatenate([p1, p1, p2, p2, p1, p3], axis=0).T.astype(jnp.bfloat16)


def rank_update(spread, scaled):
    r1, r2, r3 = split3(scaled)
    right_side = jnp.concatenate([r1, r2, r1, r2, r3, r1], axis=0).astype(jnp.bfloat16)
    return jnp.dot(spread, right_side, preferred_element_type=jnp.float32)


def negated_inverse(a_ref, matrix, between=None):
    size = matrix.shape[0]
    zero = jnp.zeros((PANEL, size), jnp.float32)
    a_ref[pl.ds(0, PANEL), :] = zero
    a_ref[pl.ds(PANEL, size), :] = matrix
    a_ref[pl.ds(PANEL + size, PANEL), :] = zero
    lane = lax.broadcasted_iota(jnp.int32, (PANEL, size), 1)
    sub = lax.broadcasted_iota(jnp.int32, (PANEL, size), 0)
    lane_full = lax.broadcasted_iota(jnp.int32, (size, size), 1)

    def columns(block, k):
        return [
            jnp.broadcast_to(
                jnp.sum(jnp.where(lane == k * PANEL + j, block, 0.0), axis=1, keepdims=True),
                block.shape,
            )
            for j in range(PANEL)
        ]

    def apply(k, spread, scaled):
        inside = (lane_full >= k * PANEL) & (lane_full < (k + 1) * PANEL)
        current = a_ref[pl.ds(PANEL, size), :]
        a_ref[pl.ds(PANEL, size), :] = jnp.where(inside, 0.0, current) - rank_update(spread, scaled)
        a_ref[pl.ds(pl.multiple_of((k + 1) * PANEL, PANEL), PANEL), :] = scaled

    def body(k, carry):
        spread_before, scaled_before, panel = carry
        apply(k - 1, spread_before, scaled_before)
        spread = spread_panel(panel)
        inside = (lane >= k * PANEL) & (lane < (k + 1) * PANEL)
        cols = columns(panel, k)
        ahead = lane == (k + 1) * PANEL + sub
        coefs = [
            jnp.broadcast_to(
                jnp.sum(
                    jnp.where(ahead, jnp.broadcast_to(panel[j : j + 1], panel.shape), 0.0),
                    axis=1, keepdims=True,
                ),
                panel.shape,
            )
            for j in range(PANEL)
        ]
        x = jnp.where(inside, jnp.where(lane - k * PANEL == sub, 1.0, 0.0), panel)
        for i in range(PANEL):
            pivot = 1.0 / jnp.broadcast_to(cols[i][i : i + 1], x.shape)
            here = sub == i

            def step(v):
                row = jnp.broadcast_to(v[i : i + 1], v.shape) * pivot
                return jnp.where(here, row, v - cols[i] * row)

            x_new = step(x)
            for j in range(i + 1, PANEL):
                cols[j] = step(cols[j])
            x = x_new
        scaled = jnp.where(inside, -x, x)
        following = a_ref[pl.ds(pl.multiple_of((k + 2) * PANEL, PANEL), PANEL), :]
        panel_next = jnp.where(inside, 0.0, following)
        for j in range(PANEL):
            panel_next = panel_next - coefs[j] * jnp.broadcast_to(scaled[j : j + 1], x.shape)
        return spread, scaled, panel_next

    steps = size // PANEL
    carry = (spread_panel(zero), zero, matrix[:PANEL])
    if between is None:
        spread, scaled, _ = lax.fori_loop(0, steps, body, carry)
    else:
        carry = lax.fori_loop(0, steps // 2, body, carry)
        between()
        spread, scaled, _ = lax.fori_loop(steps // 2, steps, body, carry)
    apply(steps - 1, spread, scaled)
    return a_ref[pl.ds(PANEL, size), :]


def dot_nt(left_hand, right_rows):
    return lax.dot_general(
        left_hand, right_rows, (((1,), (1,)), ((), ())),
        precision=lax.Precision.HIGHEST, preferred_element_type=jnp.float32,
    )


def pack(matrix):
    half, size = matrix.shape[0] // 2, matrix.shape[1]
    lane = lax.broadcasted_iota(jnp.int32, (half, size), 1)
    row = lax.broadcasted_iota(jnp.int32, (half, size), 0)
    bottom = pltpu.roll(matrix[half:], half, 1)
    main = jnp.where(lane < row, bottom, matrix[:half])
    diagonal = jnp.sum(jnp.where(lane == row, bottom, 0.0), axis=0, keepdims=True)
    return main, jnp.broadcast_to(diagonal, (PANEL, size))


def unpack(main, diagonal):
    half, size = main.shape
    lane = lax.broadcasted_iota(jnp.int32, (half, size), 1)
    row = lax.broadcasted_iota(jnp.int32, (half, size), 0)
    flipped = jnp.concatenate([main, main], axis=0).T
    top = jnp.where(lane < row, flipped[:half], main)
    lower = jnp.where(lane < row, main, flipped[:half])
    lower = jnp.where(lane == row, jnp.broadcast_to(diagonal[:1], lower.shape), lower)
    bottom = jnp.where(lane < half, flipped[half:], pltpu.roll(lower, half, 1))
    return jnp.concatenate([top, bottom], axis=0)


FF, MF, MM, CF, CM, YF, YM, CC, YC = range(9)
SYMMETRIC = (FF, MM)
LATER = (CM, CC, YF, YM, YC)
PIECES = (CM, YM, CC, YC)


def kernel(
    n_leaf, n_mid, n_top,
    prec_hbm, fine_hbm, mid_hbm, coarse_hbm, core_fine_hbm, core_mid_hbm, core_coarse_hbm, obs_hbm,
    out_ref,
    in_ref, a_ref, s_ref, raw_ref, bulk_ref, piece_in, gram_in, total_ref, down_ref, cross_ref, cross_in, last_ref,
    in_sem, piece_send, piece_recv, gram_send, gram_recv, down_send, down_recv,
    cross_send, cross_recv, last_send, last_recv, swap_send,
):
    r = bulk_ref.shape[1]
    packed = r // 2 + PANEL
    leaf, mid, top = lax.axis_index("leaf"), lax.axis_index("mid"), lax.axis_index("top")
    low, high = (n_leaf - 1) // 2, n_leaf // 2
    root = low + lax.rem(top, 2) * (high - low)
    is_root = leaf == root
    is_other = leaf != root
    side = (leaf > root).astype(jnp.int32)
    inner, outer = leaf + 1 - 2 * side, leaf - 1 + 2 * side
    has_outer = is_other & (outer >= 0) & (outer < n_leaf)
    inner_is_other = is_other & (inner != root)
    barrier = pltpu.get_barrier_semaphore()

    def greet(device):
        pl.semaphore_signal(barrier, inc=1, device_id=device, device_id_type=MESH)

    leaf_steps = sorted(range(1, n_leaf), key=lambda step: (abs(2 * step - n_leaf), step))
    peers = [(a, b) for a in range(n_mid) for b in range(n_top) if (a, b) != (0, 0)]

    def beside(a, b):
        return {"mid": lax.rem(mid + a, n_mid), "top": lax.rem(top + b, n_top)}

    def leaf_at(step):
        return {"leaf": lax.rem(leaf + step, n_leaf)}

    for a, b in peers:
        greet(beside(a, b))

    @pl.when(is_root)
    def _():
        for step in leaf_steps:
            greet(leaf_at(step))

    @pl.when(is_other)
    def _():
        greet({"leaf": root})

    @pl.when(has_outer)
    def _():
        greet({"leaf": outer})

    @pl.when(inner_is_other)
    def _():
        greet({"leaf": inner})

    sources = [prec_hbm, fine_hbm, mid_hbm, coarse_hbm, obs_hbm, core_fine_hbm, core_mid_hbm, core_coarse_hbm]
    loads = [pltpu.make_async_copy(src, in_ref.at[k], in_sem.at[k]) for k, src in enumerate(sources)]
    for load in loads:
        load.start()

    def fetch(k):
        loads[k].wait()
        return in_ref[k]

    def meet():
        around = jnp.where(is_root, n_leaf - 1, 1 + has_outer.astype(jnp.int32) + inner_is_other.astype(jnp.int32))
        pl.semaphore_wait(barrier, len(peers) + around)

    def parts(block):
        return n_mid if block in (CM, YM) else n_mid * n_top

    def height(block):
        if block in SYMMETRIC:
            return packed
        return r // parts(block) if block in PIECES else r

    def gram_copy(block, slot):
        place = slice(0, height(block))
        return pltpu.make_async_remote_copy(
            src_ref=bulk_ref.at[block, place], dst_ref=gram_in.at[slot, block, place],
            send_sem=gram_send.at[block], recv_sem=gram_recv.at[slot, block],
            device_id={"leaf": root}, device_id_type=MESH,
        )

    slot_here = lax.rem(root - leaf + n_leaf, n_leaf) - 1

    def store(ref, block, value, symmetric):
        if symmetric:
            main, diagonal = pack(value)
            ref[block, : r // 2] = main
            ref[block, r // 2 : packed] = diagonal
        else:
            ref[block] = value

    def piece_copy(block, number):
        a, b = peers[number]
        count, rows = parts(block), r // parts(block)
        there = beside(a, b)
        index = there["mid"] if count == n_mid else there["mid"] * n_top + there["top"]
        return pltpu.make_async_remote_copy(
            src_ref=raw_ref.at[PIECES.index(block), pl.ds(pl.multiple_of(index * rows, PANEL), rows)],
            dst_ref=piece_in.at[number, PIECES.index(block), slice(0, rows)],
            send_sem=piece_send.at[number, PIECES.index(block)], recv_sem=piece_recv.at[number, PIECES.index(block)],
            device_id=there, device_id_type=MESH,
        )

    def sharers(block):
        return [k for k, (a, b) in enumerate(peers) if b == 0 or parts(block) != n_mid]

    def own_place(block):
        rows = r // parts(block)
        index = mid if parts(block) == n_mid else mid * n_top + top
        return pl.ds(pl.multiple_of(index * rows, PANEL), rows)

    def share(block, value):
        raw_ref[PIECES.index(block)] = value
        for number in sharers(block):
            piece_copy(block, number).start()

    def join(block):
        k = PIECES.index(block)
        total = raw_ref[k, own_place(block)]
        for number in sharers(block):
            piece_copy(block, number).wait_recv()
            total = total + piece_in[number, k, : r // parts(block)]
        bulk_ref[block, : r // parts(block)] = total

    def give(block, value):
        store(bulk_ref, block, value, block in SYMMETRIC)

        if block not in LATER:
            @pl.when(is_other)
            def _():
                gram_copy(block, slot_here).start()

    prec, fine = fetch(0), fetch(1)
    solved_f = dot(prec, fine)
    s_ref[0] = solved_f
    gram_ff = dot(fine.T, solved_f)
    meet()
    give(FF, gram_ff)
    middle = fetch(2)
    mid_t = middle.T
    give(MF, dot(mid_t, solved_f))
    solved_m = dot(prec, middle)
    s_ref[1] = solved_m
    give(MM, dot(mid_t, solved_m))
    coarse = fetch(3)
    coarse_t = coarse.T
    give(CF, dot(coarse_t, solved_f))
    share(CM, dot(coarse_t, solved_m))
    solved_c = dot(prec, coarse)
    s_ref[2] = solved_c
    share(CC, dot(coarse_t, solved_c))
    obs = fetch(4)
    obs_t = obs.T
    share(YM, dot(obs_t, solved_m))
    share(YC, dot(obs_t, solved_c))
    give(YF, dot(obs_t, solved_f))
    s_ref[3] = dot(prec, obs)
    for k in range(5, 8):
        loads[k].wait()

    def gathered(block):
        place = slice(0, height(block))
        if block in PIECES:
            join(block)
        total = bulk_ref[block, place]
        for slot in range(n_leaf - 1):
            gram_copy(block, slot).wait_recv()
            total = total + gram_in[slot, block, place]
        return total

    def whole(value):
        return unpack(value[: r // 2], value[r // 2 :])

    def down_copy(block, slot, target):
        return pltpu.make_async_remote_copy(
            src_ref=down_ref.at[block], dst_ref=down_ref.at[block],
            send_sem=down_send.at[block, slot], recv_sem=down_recv.at[block],
            device_id={"leaf": target}, device_id_type=MESH,
        )

    def send_down(block, value):
        down_ref[block] = value
        for slot, exists in enumerate((root > 0, root < n_leaf - 1)):
            def go():
                down_copy(block, slot, root + 2 * slot - 1).start()

            if n_leaf > 2:
                go()
            else:
                pl.when(exists)(go)

    def pass_on(block):
        down_copy(block, 0, outer).wait_recv()

        @pl.when(has_outer)
        def _():
            down_copy(block, 0, outer).start()

    def cross_place(block):
        return slice(0, packed if block in (0, 3) else r)

    def cross_copy(block, step):
        return pltpu.make_async_remote_copy(
            src_ref=cross_ref.at[block, cross_place(block)], dst_ref=cross_in.at[step - 1, block, cross_place(block)],
            send_sem=cross_send.at[block, step - 1], recv_sem=cross_recv.at[block, step - 1],
            device_id={"mid": lax.rem(mid + step, n_mid)}, device_id_type=MESH,
        )

    def cross_start(block):
        for step in range(1, n_mid):
            cross_copy(block, step).start()

    def crossed(block):
        total = cross_ref[block, cross_place(block)]
        for step in range(1, n_mid):
            cross_copy(block, step).wait_recv()
            total = total + cross_in[step - 1, block, cross_place(block)]
        return total

    def corrected(raw, left_hand, right_rows):
        total_ref[...] = dot_nt(left_hand, right_rows)
        piece = gathered(raw)
        total_ref[own_place(raw)] = total_ref[own_place(raw)] + piece
        return total_ref[...]

    def last_place(block):
        return slice(0, r if block else packed)

    def last_copy(block, step):
        return pltpu.make_async_remote_copy(
            src_ref=last_ref.at[top, block, last_place(block)], dst_ref=last_ref.at[top, block, last_place(block)],
            send_sem=last_send.at[block, step - 1], recv_sem=last_recv.at[block, top],
            device_id=leaf_at(step), device_id_type=MESH,
        )

    def swap_copy(block, source, step):
        return pltpu.make_async_remote_copy(
            src_ref=last_ref.at[source, block, last_place(block)], dst_ref=last_ref.at[source, block, last_place(block)],
            send_sem=swap_send.at[block, step - 1], recv_sem=last_recv.at[block, source],
            device_id={"top": lax.rem(top + step, n_top)}, device_id_type=MESH,
        )

    def swap(block):
        for step in range(1, n_top):
            swap_copy(block, top, step).start()

    def send_last(block):
        for step in leaf_steps:
            last_copy(block, step).start()
        swap(block)

    def after_fine():
        s_ref[1] = s_ref[1] + dot_nt(s_ref[0], down_ref[0])
        s_ref[2] = s_ref[2] + dot_nt(s_ref[0], down_ref[1])

    @pl.when(is_root)
    def _():
        inverse = negated_inverse(a_ref, in_ref[5] + whole(gathered(FF)))
        mf = gathered(MF)
        n_m = dot(mf, inverse)
        store(cross_ref, 0, whole(gathered(MM)) + dot_nt(n_m, mf), True)
        cross_start(0)
        cf = gathered(CF)
        n_c = dot(cf, inverse)
        cross_ref[1] = corrected(CM, n_c, mf)
        cross_start(1)
        store(cross_ref, 3, corrected(CC, n_c, cf), True)
        cross_start(3)
        send_down(0, n_m)
        send_down(1, n_c)
        after_fine()
        n_y = dot(gathered(YF), inverse)
        cross_ref[2] = corrected(YM, n_y, mf)
        cross_start(2)
        cross_ref[4] = corrected(YC, n_y, cf)
        cross_start(4)
        send_down(2, n_y)

        inverse = negated_inverse(a_ref, in_ref[6] + whole(crossed(0)))
        cm = crossed(1)
        q_c = dot(cm, inverse)
        store(last_ref.at[top], 0, whole(crossed(3)) + dot_nt(q_c, cm), True)
        send_last(0)
        q_y = dot(crossed(2), inverse)
        last_ref[top, 1] = crossed(4) + dot_nt(q_y, cm)
        send_last(1)
        send_down(3, q_c)
        send_down(4, q_y)

    @pl.when(is_other)
    def _():
        for block in LATER:
            if block in PIECES:
                join(block)
            gram_copy(block, slot_here).start()
        pass_on(0)
        pass_on(1)
        pass_on(2)
        after_fine()
        last_copy(0, 1).wait_recv()
        swap(0)

    def others_arrived(block):
        for step in range(1, n_top):
            swap_copy(block, lax.rem(top + step, n_top), step).wait_recv()

    others_arrived(0)
    coarse_sum = last_ref[0, 0, :packed]
    for t in range(1, n_top):
        coarse_sum = coarse_sum + last_ref[t, 0, :packed]

    def middle_of_inverse():
        @pl.when(is_other)
        def _():
            last_copy(1, 1).wait_recv()
            swap(1)
            pass_on(3)

    inverse = negated_inverse(a_ref, in_ref[7] + whole(coarse_sum), middle_of_inverse)

    @pl.when(is_other)
    def _():
        pass_on(4)

    after_m = s_ref[1]
    after_c = s_ref[2] + dot_nt(after_m, down_ref[3])
    after_y = s_ref[3] + dot_nt(s_ref[0], down_ref[2]) + dot_nt(after_m, down_ref[4])
    others_arrived(1)
    right = last_ref[0, 1]
    for t in range(1, n_top):
        right = right + last_ref[t, 1]
    out_ref[...] = after_y + dot_nt(after_c, dot(right, inverse))

    for block in PIECES:
        for number in sharers(block):
            piece_copy(block, number).wait_send()
    for block in range(2):
        for step in range(1, n_top):
            swap_copy(block, top, step).wait_send()

    @pl.when(is_root)
    def _():
        for block in range(5):
            for step in range(1, n_mid):
                cross_copy(block, step).wait_send()
            for slot, exists in enumerate((root > 0, root < n_leaf - 1)):
                def done():
                    down_copy(block, slot, root + 2 * slot - 1).wait_send()

                if n_leaf > 2:
                    done()
                else:
                    pl.when(exists)(done)
        for block in range(2):
            for step in leaf_steps:
                last_copy(block, step).wait_send()

    @pl.when(is_other)
    def _():
        for block in range(9):
            gram_copy(block, slot_here).wait_send()

    @pl.when(has_outer)
    def _():
        for block in range(5):
            down_copy(block, 0, outer).wait_send()


def local(n_leaf, n_mid, n_top, *operands):
    blocks = [x.reshape(x.shape[-2:]) for x in operands]
    r = blocks[1].shape[1]
    f32 = jnp.float32
    dma = pltpu.SemaphoreType.DMA
    beside = max(n_mid * n_top - 1, 1)
    answer = pl.pallas_call(
        functools.partial(kernel, n_leaf, n_mid, n_top),
        out_shape=jax.ShapeDtypeStruct(blocks[-1].shape, f32),
        in_specs=[pl.BlockSpec(memory_space=pl.ANY)] * len(blocks),
        out_specs=pl.BlockSpec(memory_space=pltpu.VMEM),
        scratch_shapes=[
            pltpu.VMEM((8, r, r), f32),
            pltpu.VMEM((r + 2 * PANEL, r), f32),
            pltpu.VMEM((4, r, r), f32),
            pltpu.VMEM((4, r, r), f32),
            pltpu.VMEM((9, r, r), f32),
            pltpu.VMEM((beside, 4, r // n_mid, r), f32),
            pltpu.VMEM((n_leaf - 1, 9, r, r), f32),
            pltpu.VMEM((r, r), f32),
            pltpu.VMEM((5, r, r), f32),
            pltpu.VMEM((5, r, r), f32),
            pltpu.VMEM((n_mid - 1, 5, r, r), f32),
            pltpu.VMEM((n_top, 2, r, r), f32),
            dma((8,)),
            dma((beside, 4)), dma((beside, 4)),
            dma((9,)), dma((n_leaf - 1, 9)),
            dma((5, 2)), dma((5,)),
            dma((5, n_mid - 1)), dma((5, n_mid - 1)),
            dma((2, n_leaf - 1)), dma((2, n_top)), dma((2, n_top - 1)),
        ],
        compiler_params=pltpu.CompilerParams(collective_id=0, has_side_effects=True),
    )(*blocks)
    return answer[None, None, None]


def solution(mesh):
    spread = P(("parts", "leaf"), "mid", "top", None, None)
    sizes = (mesh.shape["leaf"], mesh.shape["mid"], mesh.shape["top"])
    return jax.shard_map(
        functools.partial(local, *sizes),
        mesh=mesh,
        in_specs=(spread, spread, spread, spread, P(), P(), P(), spread),
        out_specs=spread,
        check_vma=False,
    )
```

time: 34.2 us -> 31.1 us (0.909)
  the two profiles are of different devices: /device:TPU:0 before, /device:TPU:24 now
where the time goes in v2:
time: 31.1 us; the launch traced here: 30.9 us
  Pallas kernels  29.4 us (95%)
  local copies, waits for them, and re-layouts  1.47 us (5%)
    pallas_call x1, Pallas kernels, local(): pl.pallas_call(functools.partial(kernel, n_leaf, n_mid, n_top), out_shape...  29.4 us
    unnamed x1, local copies, waits for them, and re-layouts  1.47 us

profile of v2, /device:TPU:24, one launch (start us, length us, event | category | flops | bytes accessed | tf_op | source)
XLA Modules:
  0.0 30.9 jit_solution(11253744459979500593)
XLA Ops:
  0.0 29.4 %shard_map.82 = f32[128,128]{1,0:T(8,128)} custom-call(f32[128,128]{1,0:T(8,128)} %bitcast.7, f32[128,128]{1,0:T(8,128)} %bitcast.8, f32[128,128]{1,0:T(8,128)} %bitcast.9, f32[128,128]{1,0:T(8,128)} %bitcast.10, f32[128,128]{1,0:T(8,128)} %core_fine_hbm.1, f32[128,128]{1,0:T(8,128)} %core_mid_hbm.1, f32[128,128]{1,0:T(8,128)} %core_coarse_hbm.1, ...), custom_call_target="tpu_custom_call" | custom-call | tf_op jit(solution)/shard_map/pallas_call | solution.py:523
  29.4 1.5 %copy.10 = f32[1,1,1,128,128]{4,3,2,1,0:T(8,128)} copy(f32[1,1,1,128,128]{4,3,2,1,0:T(8,128)} %bitcast.6) | data formatting | bytes 131072

commit v3 on v2

--- a/solution.py
+++ b/solution.py
@@ -9,6 +9,7 @@
 
 MESH = pl.DeviceIdType.MESH
 PANEL = 8
+VMEM_ROOM = 56_558_000
 
 
 def dot(left_hand, right_side):
@@ -46,14 +47,12 @@
     sub = lax.broadcasted_iota(jnp.int32, (PANEL, size), 0)
     lane_full = lax.broadcasted_iota(jnp.int32, (size, size), 1)
 
-    def columns(block, k):
-        return [
-            jnp.broadcast_to(
-                jnp.sum(jnp.where(lane == k * PANEL + j, block, 0.0), axis=1, keepdims=True),
-                block.shape,
-            )
-            for j in range(PANEL)
-        ]
+    def lanes(block, index):
+        picked = jnp.where(lane == index, block, 0.0)
+        return jnp.broadcast_to(jnp.sum(picked, axis=1, keepdims=True), block.shape)
+
+    def row_of(block, i):
+        return jnp.broadcast_to(block[i : i + 1], block.shape)
 
     def apply(k, spread, scaled):
         inside = (lane_full >= k * PANEL) & (lane_full < (k + 1) * PANEL)
@@ -64,39 +63,33 @@
     def body(k, carry):
         spread_before, scaled_before, panel = carry
         apply(k - 1, spread_before, scaled_before)
+        inside = (lane >= k * PANEL) & (lane < (k + 1) * PANEL)
+        cols = [lanes(panel, k * PANEL + j) for j in range(PANEL)]
+        ahead = (k + 1) * PANEL + sub
+        below = [lanes(row_of(panel, j), ahead) for j in range(PANEL)]
         spread = spread_panel(panel)
-        inside = (lane >= k * PANEL) & (lane < (k + 1) * PANEL)
-        cols = columns(panel, k)
-        ahead = lane == (k + 1) * PANEL + sub
-        coefs = [
-            jnp.broadcast_to(
-                jnp.sum(
-                    jnp.where(ahead, jnp.broadcast_to(panel[j : j + 1], panel.shape), 0.0),
-                    axis=1, keepdims=True,
-                ),
-                panel.shape,
-            )
-            for j in range(PANEL)
-        ]
+        following = a_ref[pl.ds(pl.multiple_of((k + 2) * PANEL, PANEL), PANEL), :]
         x = jnp.where(inside, jnp.where(lane - k * PANEL == sub, 1.0, 0.0), panel)
+        gone = jnp.zeros_like(x)
+        scale = gone
         for i in range(PANEL):
-            pivot = 1.0 / jnp.broadcast_to(cols[i][i : i + 1], x.shape)
+            pivot = 1.0 / row_of(cols[i], i)
             here = sub == i
-
-            def step(v):
-                row = jnp.broadcast_to(v[i : i + 1], v.shape) * pivot
-                return jnp.where(here, row, v - cols[i] * row)
-
-            x_new = step(x)
+            factor = jnp.where(here, 0.0, cols[i])
+            row = row_of(x, i)
+            across, down = factor * pivot, below[i] * pivot
             for j in range(i + 1, PANEL):
-                cols[j] = step(cols[j])
-            x = x_new
-        scaled = jnp.where(inside, -x, x)
-        following = a_ref[pl.ds(pl.multiple_of((k + 2) * PANEL, PANEL), PANEL), :]
-        panel_next = jnp.where(inside, 0.0, following)
-        for j in range(PANEL):
-            panel_next = panel_next - coefs[j] * jnp.broadcast_to(scaled[j : j + 1], x.shape)
-        return spread, scaled, panel_next
+                entry = row_of(cols[j], i)
+                if j == i + 1:
+                    cols[j] = cols[j] - (factor * entry) * pivot
+                else:
+                    cols[j] = cols[j] - across * entry
+                below[j] = below[j] - down * entry
+            x = x - across * row
+            gone = gone + down * row
+            scale = jnp.where(here, pivot, scale)
+        x = x * scale
+        return spread, jnp.where(inside, -x, x), jnp.where(inside, gone, following - gone)
 
     steps = size // PANEL
     carry = (spread_panel(zero), zero, matrix[:PANEL])
@@ -119,45 +112,46 @@
 
 def pack(matrix):
     half, size = matrix.shape[0] // 2, matrix.shape[1]
-    lane = lax.broadcasted_iota(jnp.int32, (half, size), 1)
-    row = lax.broadcasted_iota(jnp.int32, (half, size), 0)
-    bottom = pltpu.roll(matrix[half:], half, 1)
-    main = jnp.where(lane < row, bottom, matrix[:half])
-    diagonal = jnp.sum(jnp.where(lane == row, bottom, 0.0), axis=0, keepdims=True)
-    return main, jnp.broadcast_to(diagonal, (PANEL, size))
-
-
-def unpack(main, diagonal):
-    half, size = main.shape
-    lane = lax.broadcasted_iota(jnp.int32, (half, size), 1)
-    row = lax.broadcasted_iota(jnp.int32, (half, size), 0)
-    flipped = jnp.concatenate([main, main], axis=0).T
-    top = jnp.where(lane < row, flipped[:half], main)
-    lower = jnp.where(lane < row, main, flipped[:half])
-    lower = jnp.where(lane == row, jnp.broadcast_to(diagonal[:1], lower.shape), lower)
-    bottom = jnp.where(lane < half, flipped[half:], pltpu.roll(lower, half, 1))
-    return jnp.concatenate([top, bottom], axis=0)
+    lane = lax.broadcasted_iota(jnp.int32, (PANEL, size), 1)
+    blocks = [matrix[:PANEL]]
+    for start in range(PANEL, half + 1, PANEL):
+        moved = pltpu.roll(matrix[size - start : size - start + PANEL], start, 1)
+        blocks.append(moved if start == half else jnp.where(lane < start, moved, matrix[start : start + PANEL]))
+    return jnp.concatenate(blocks, axis=0)
+
+
+def unpack(packed):
+    half, size = packed.shape[0] - PANEL, packed.shape[1]
+    bottom = [pltpu.roll(packed[start : start + PANEL], size - start, 1) for start in range(half, 0, -PANEL)]
+    return jnp.concatenate([packed[:half], *bottom], axis=0)
 
 
 FF, MF, MM, CF, CM, YF, YM, CC, YC = range(9)
 SYMMETRIC = (FF, MM)
 LATER = (CM, CC, YF, YM, YC)
 PIECES = (CM, YM, CC, YC)
+SEEN = (YF, YM, YC)
 
 
 def kernel(
     n_leaf, n_mid, n_top,
     prec_hbm, fine_hbm, mid_hbm, coarse_hbm, core_fine_hbm, core_mid_hbm, core_coarse_hbm, obs_hbm,
     out_ref,
-    in_ref, a_ref, s_ref, raw_ref, bulk_ref, piece_in, gram_in, total_ref, down_ref, cross_ref, cross_in, last_ref,
-    in_sem, piece_send, piece_recv, gram_send, gram_recv, down_send, down_recv,
-    cross_send, cross_recv, last_send, last_recv, swap_send,
+    in_ref, a_ref, s_ref, raw_ref, bulk_ref, piece_in, gram_in, total_ref, kept_ref, down_ref, cross_ref, cross_in, last_ref, seen_in, answer_ref,
+    in_sem, piece_send, piece_recv, gram_send, gram_recv, down_send, down_recv, spread_send,
+    cross_send, cross_recv, last_send, last_recv, swap_send, seen_recv, help_send, help_recv, answer_send,
 ):
     r = bulk_ref.shape[1]
     packed = r // 2 + PANEL
     leaf, mid, top = lax.axis_index("leaf"), lax.axis_index("mid"), lax.axis_index("top")
     low, high = (n_leaf - 1) // 2, n_leaf // 2
-    root = low + lax.rem(top, 2) * (high - low)
+
+    def root_of(index):
+        return low + lax.rem(index, 2) * (high - low)
+
+    root = root_of(top)
+    after_top, before_top = lax.rem(top + 1, n_top), lax.rem(top + n_top - 1, n_top)
+    is_helper = leaf == root_of(before_top)
     is_root = leaf == root
     is_other = leaf != root
     side = (leaf > root).astype(jnp.int32)
@@ -190,6 +184,13 @@
     def _():
         greet({"leaf": root})
 
+        greet({"leaf": root, "top": after_top})
+
+    @pl.when(is_helper)
+    def _():
+        for step in leaf_steps:
+            greet({**leaf_at(step), "top": before_top})
+
     @pl.when(has_outer)
     def _():
         greet({"leaf": outer})
@@ -208,8 +209,9 @@
         return in_ref[k]
 
     def meet():
-        around = jnp.where(is_root, n_leaf - 1, 1 + has_outer.astype(jnp.int32) + inner_is_other.astype(jnp.int32))
-        pl.semaphore_wait(barrier, len(peers) + around)
+        around = jnp.where(is_root, n_leaf - 1, 2 + has_outer.astype(jnp.int32) + inner_is_other.astype(jnp.int32))
+        helped = jnp.where(is_helper, n_leaf - 1, 0)
+        pl.semaphore_wait(barrier, len(peers) + around + helped)
 
     def parts(block):
         return n_mid if block in (CM, YM) else n_mid * n_top
@@ -229,11 +231,17 @@
 
     slot_here = lax.rem(root - leaf + n_leaf, n_leaf) - 1
 
+    def seen_copy(block, slot):
+        place = slice(0, height(block))
+        return pltpu.make_async_remote_copy(
+            src_ref=bulk_ref.at[block, place], dst_ref=seen_in.at[slot, SEEN.index(block), place],
+            send_sem=gram_send.at[block], recv_sem=seen_recv.at[slot, SEEN.index(block)],
+            device_id={"leaf": root, "top": after_top}, device_id_type=MESH,
+        )
+
     def store(ref, block, value, symmetric):
         if symmetric:
-            main, diagonal = pack(value)
-            ref[block, : r // 2] = main
-            ref[block, r // 2 : packed] = diagonal
+            ref[block, :packed] = pack(value)
         else:
             ref[block] = value
 
@@ -252,9 +260,9 @@
     def sharers(block):
         return [k for k, (a, b) in enumerate(peers) if b == 0 or parts(block) != n_mid]
 
-    def own_place(block):
+    def own_place(block, group):
         rows = r // parts(block)
-        index = mid if parts(block) == n_mid else mid * n_top + top
+        index = mid if parts(block) == n_mid else mid * n_top + group
         return pl.ds(pl.multiple_of(index * rows, PANEL), rows)
 
     def share(block, value):
@@ -264,7 +272,7 @@
 
     def join(block):
         k = PIECES.index(block)
-        total = raw_ref[k, own_place(block)]
+        total = raw_ref[k, own_place(block, top)]
         for number in sharers(block):
             piece_copy(block, number).wait_recv()
             total = total + piece_in[number, k, : r // parts(block)]
@@ -316,9 +324,6 @@
             total = total + gram_in[slot, block, place]
         return total
 
-    def whole(value):
-        return unpack(value[: r // 2], value[r // 2 :])
-
     def down_copy(block, slot, target):
         return pltpu.make_async_remote_copy(
             src_ref=down_ref.at[block], dst_ref=down_ref.at[block],
@@ -337,12 +342,61 @@
             else:
                 pl.when(exists)(go)
 
+    def spread_copy(block, step):
+        return pltpu.make_async_remote_copy(
+            src_ref=down_ref.at[block], dst_ref=down_ref.at[block],
+            send_sem=spread_send.at[block - 3, step - 1], recv_sem=down_recv.at[block],
+            device_id=leaf_at(step), device_id_type=MESH,
+        )
+
+    def send_all(block, value):
+        down_ref[block] = value
+        for step in leaf_steps:
+            spread_copy(block, step).start()
+
     def pass_on(block):
         down_copy(block, 0, outer).wait_recv()
 
         @pl.when(has_outer)
         def _():
             down_copy(block, 0, outer).start()
+
+    def seen(block):
+        place = slice(0, height(block))
+        for slot in range(n_leaf):
+            seen_copy(block, slot).wait_recv()
+        total = seen_in[0, SEEN.index(block), place]
+        for slot in range(1, n_leaf):
+            total = total + seen_in[slot, SEEN.index(block), place]
+        return total
+
+    def help_copy(number):
+        return pltpu.make_async_remote_copy(
+            src_ref=kept_ref.at[number], dst_ref=kept_ref.at[number],
+            send_sem=help_send.at[number], recv_sem=help_recv.at[number],
+            device_id={"top": after_top}, device_id_type=MESH,
+        )
+
+    def keep(number, value):
+        kept_ref[number] = value
+        help_copy(number).start()
+
+    def answer_copy(number, step):
+        target, arrival = (
+            (down_ref.at[2], down_recv.at[2]),
+            (last_ref.at[before_top, 1], last_recv.at[1, before_top]),
+            (down_ref.at[4], down_recv.at[4]),
+        )[number]
+        return pltpu.make_async_remote_copy(
+            src_ref=answer_ref.at[number], dst_ref=target,
+            send_sem=answer_send.at[number, step], recv_sem=arrival,
+            device_id={**leaf_at(step), "top": before_top}, device_id_type=MESH,
+        )
+
+    def send_answer(number, value):
+        answer_ref[number] = value
+        for step in [*leaf_steps, 0]:
+            answer_copy(number, step).start()
 
     def cross_place(block):
         return slice(0, packed if block in (0, 3) else r)
@@ -365,10 +419,10 @@
             total = total + cross_in[step - 1, block, cross_place(block)]
         return total
 
-    def corrected(raw, left_hand, right_rows):
-        total_ref[...] = dot_nt(left_hand, right_rows)
-        piece = gathered(raw)
-        total_ref[own_place(raw)] = total_ref[own_place(raw)] + piece
+    def corrected(raw, value):
+        total_ref[...] = value
+        piece, group = (seen(raw), before_top) if raw in SEEN else (gathered(raw), top)
+        total_ref[own_place(raw, group)] = total_ref[own_place(raw, group)] + piece
         return total_ref[...]
 
     def last_place(block):
@@ -400,50 +454,82 @@
     def after_fine():
         s_ref[1] = s_ref[1] + dot_nt(s_ref[0], down_ref[0])
         s_ref[2] = s_ref[2] + dot_nt(s_ref[0], down_ref[1])
+        s_ref[3] = s_ref[3] + dot_nt(s_ref[0], down_ref[2])
 
     @pl.when(is_root)
     def _():
-        inverse = negated_inverse(a_ref, in_ref[5] + whole(gathered(FF)))
+        inverse = negated_inverse(a_ref, in_ref[5] + unpack(gathered(FF)))
         mf = gathered(MF)
         n_m = dot(mf, inverse)
-        store(cross_ref, 0, whole(gathered(MM)) + dot_nt(n_m, mf), True)
+        store(cross_ref, 0, unpack(gathered(MM)) + dot_nt(n_m, mf), True)
         cross_start(0)
+        keep(0, inverse)
+        keep(1, mf)
         cf = gathered(CF)
         n_c = dot(cf, inverse)
-        cross_ref[1] = corrected(CM, n_c, mf)
+        keep(2, cf)
+        lost = dot_nt(n_c, kept_ref[1:3].reshape(2 * r, r))
+        cross_ref[1] = corrected(CM, lost[:, :r])
         cross_start(1)
-        store(cross_ref, 3, corrected(CC, n_c, cf), True)
+        store(cross_ref, 3, corrected(CC, lost[:, r:]), True)
         cross_start(3)
+        for block in SEEN:
+            if block in PIECES:
+                join(block)
+            seen_copy(block, 0).start()
         send_down(0, n_m)
         send_down(1, n_c)
-        after_fine()
-        n_y = dot(gathered(YF), inverse)
-        cross_ref[2] = corrected(YM, n_y, mf)
-        cross_start(2)
-        cross_ref[4] = corrected(YC, n_y, cf)
-        cross_start(4)
-        send_down(2, n_y)
-
-        inverse = negated_inverse(a_ref, in_ref[6] + whole(crossed(0)))
+
+        inverse = negated_inverse(a_ref, in_ref[6] + unpack(crossed(0)))
         cm = crossed(1)
         q_c = dot(cm, inverse)
-        store(last_ref.at[top], 0, whole(crossed(3)) + dot_nt(q_c, cm), True)
+        store(last_ref.at[top], 0, unpack(crossed(3)) + dot_nt(q_c, cm), True)
         send_last(0)
-        q_y = dot(crossed(2), inverse)
-        last_ref[top, 1] = crossed(4) + dot_nt(q_y, cm)
-        send_last(1)
-        send_down(3, q_c)
-        send_down(4, q_y)
+        keep(3, inverse)
+        keep(4, cm)
+        send_all(3, q_c)
+        down_copy(2, 0, outer).wait_recv()
+        after_fine()
 
     @pl.when(is_other)
     def _():
         for block in LATER:
             if block in PIECES:
                 join(block)
-            gram_copy(block, slot_here).start()
+            if block in SEEN:
+                seen_copy(block, slot_here + 1).start()
+            else:
+                gram_copy(block, slot_here).start()
+
+    @pl.when(is_helper)
+    def _():
+        for number in range(2):
+            help_copy(number).wait_recv()
+        n_y = dot(seen(YF), kept_ref[0])
+        help_copy(2).wait_recv()
+        lost = dot_nt(n_y, kept_ref[1:3].reshape(2 * r, r))
+        cross_ref[2] = corrected(YM, lost[:, :r])
+        cross_start(2)
+        cross_ref[4] = corrected(YC, lost[:, r:])
+        cross_start(4)
+        send_answer(0, n_y)
+
+    @pl.when(is_other)
+    def _():
         pass_on(0)
         pass_on(1)
-        pass_on(2)
+
+    @pl.when(is_helper)
+    def _():
+        for number in range(3, 5):
+            help_copy(number).wait_recv()
+        q_y = dot(crossed(2), kept_ref[3])
+        send_answer(1, crossed(4) + dot_nt(q_y, kept_ref[4]))
+        send_answer(2, q_y)
+
+    @pl.when(is_other)
+    def _():
+        down_copy(2, 0, outer).wait_recv()
         after_fine()
         last_copy(0, 1).wait_recv()
         swap(0)
@@ -458,26 +544,22 @@
         coarse_sum = coarse_sum + last_ref[t, 0, :packed]
 
     def middle_of_inverse():
-        @pl.when(is_other)
-        def _():
-            last_copy(1, 1).wait_recv()
-            swap(1)
-            pass_on(3)
-
-    inverse = negated_inverse(a_ref, in_ref[7] + whole(coarse_sum), middle_of_inverse)
+        last_copy(1, 1).wait_recv()
+        swap(1)
+
+    inverse = negated_inverse(a_ref, in_ref[7] + unpack(coarse_sum), middle_of_inverse)
 
     @pl.when(is_other)
     def _():
-        pass_on(4)
-
-    after_m = s_ref[1]
-    after_c = s_ref[2] + dot_nt(after_m, down_ref[3])
-    after_y = s_ref[3] + dot_nt(s_ref[0], down_ref[2]) + dot_nt(after_m, down_ref[4])
+        spread_copy(3, 1).wait_recv()
+
+    spread_copy(4, 1).wait_recv()
     others_arrived(1)
     right = last_ref[0, 1]
     for t in range(1, n_top):
         right = right + last_ref[t, 1]
-    out_ref[...] = after_y + dot_nt(after_c, dot(right, inverse))
+    after = dot_nt(s_ref[1], down_ref[3:5].reshape(2 * r, r))
+    out_ref[...] = s_ref[3] + after[:, r:] + dot_nt(s_ref[2] + after[:, :r], dot(right, inverse))
 
     for block in PIECES:
         for number in sharers(block):
@@ -488,9 +570,17 @@
 
     @pl.when(is_root)
     def _():
-        for block in range(5):
+        for block in (0, 1, 3):
             for step in range(1, n_mid):
                 cross_copy(block, step).wait_send()
+        for step in leaf_steps:
+            spread_copy(3, step).wait_send()
+            last_copy(0, step).wait_send()
+        for number in range(5):
+            help_copy(number).wait_send()
+        for block in SEEN:
+            seen_copy(block, 0).wait_send()
+        for block in range(2):
             for slot, exists in enumerate((root > 0, root < n_leaf - 1)):
                 def done():
                     down_copy(block, slot, root + 2 * slot - 1).wait_send()
@@ -499,9 +589,15 @@
                     done()
                 else:
                     pl.when(exists)(done)
-        for block in range(2):
-            for step in leaf_steps:
-                last_copy(block, step).wait_send()
+
+    @pl.when(is_helper)
+    def _():
+        for block in (2, 4):
+            for step in range(1, n_mid):
+                cross_copy(block, step).wait_send()
+        for number in range(3):
+            for step in range(n_leaf):
+                answer_copy(number, step).wait_send()
 
     @pl.when(is_other)
     def _():
@@ -510,7 +606,7 @@
 
     @pl.when(has_outer)
     def _():
-        for block in range(5):
+        for block in range(2):
             down_copy(block, 0, outer).wait_send()
 
 
@@ -536,16 +632,22 @@
             pltpu.VMEM((r, r), f32),
             pltpu.VMEM((5, r, r), f32),
             pltpu.VMEM((5, r, r), f32),
+            pltpu.VMEM((5, r, r), f32),
             pltpu.VMEM((n_mid - 1, 5, r, r), f32),
             pltpu.VMEM((n_top, 2, r, r), f32),
+            pltpu.VMEM((n_leaf, 3, r, r), f32),
+            pltpu.VMEM((3, r, r), f32),
             dma((8,)),
             dma((beside, 4)), dma((beside, 4)),
             dma((9,)), dma((n_leaf - 1, 9)),
-            dma((5, 2)), dma((5,)),
+            dma((3, 2)), dma((5,)), dma((2, n_leaf - 1)),
             dma((5, n_mid - 1)), dma((5, n_mid - 1)),
             dma((2, n_leaf - 1)), dma((2, n_top)), dma((2, n_top - 1)),
+            dma((n_leaf, 3)), dma((5,)), dma((5,)), dma((3, n_leaf)),
         ],
-        compiler_params=pltpu.CompilerParams(collective_id=0, has_side_effects=True),
+        compiler_params=pltpu.CompilerParams(
+            collective_id=0, has_side_effects=True, vmem_limit_bytes=VMEM_ROOM - 3 * r * blocks[-1].shape[1] * 2,
+        ),
     )(*blocks)
     return answer[None, None, None]
 

time: 31.1 us -> 28.4 us (0.913)
  the two profiles are of different devices: /device:TPU:24 before, /device:TPU:0 now
where the time goes in v3:
time: 28.4 us; the launch traced here: 28.3 us
  Pallas kernels  27.6 us (97%)
  local copies, waits for them, and re-layouts  0.63 us (2%)
    pallas_call x1, Pallas kernels, local(): pl.pallas_call(functools.partial(kernel, n_leaf, n_mid, n_top), out_shape...  27.6 us
    unnamed x1, local copies, waits for them, and re-layouts  0.63 us

profile of v3, /device:TPU:0, one launch (start us, length us, event | category | flops | bytes accessed | tf_op | source)
XLA Modules:
  0.0 28.3 jit_solution(8410894247135519254)
XLA Ops:
  0.0 27.6 %shard_map.82 = f32[128,128]{1,0:T(8,128)S(1)} custom-call(f32[128,128]{1,0:T(8,128)} %bitcast.7, f32[128,128]{1,0:T(8,128)} %bitcast.8, f32[128,128]{1,0:T(8,128)} %bitcast.9, f32[128,128]{1,0:T(8,128)} %bitcast.10, f32[128,128]{1,0:T(8,128)} %core_fine_hbm.1, f32[128,128]{1,0:T(8,128)} %core_mid_hbm.1, f32[128,128]{1,0:T(8,128)} %core_coarse_hbm.1, ...), custom_call_target="tpu_custom_call" | custom-call | tf_op jit(solution)/shard_map/pallas_call | solution.py:619
  27.7 0.6 %copy.10 = f32[1,1,1,128,128]{4,3,2,1,0:T(8,128)} copy(f32[1,1,1,128,128]{4,3,2,1,0:T(8,128)S(1)} %bitcast.6) | data formatting | bytes 131072

commit v4 on v3

--- a/solution.py
+++ b/solution.py
@@ -356,10 +356,7 @@
 
     def pass_on(block):
         down_copy(block, 0, outer).wait_recv()
-
-        @pl.when(has_outer)
-        def _():
-            down_copy(block, 0, outer).start()
+        down_copy(block, 0, outer).start()
 
     def seen(block):
         place = slice(0, height(block))
@@ -463,6 +460,7 @@
         n_m = dot(mf, inverse)
         store(cross_ref, 0, unpack(gathered(MM)) + dot_nt(n_m, mf), True)
         cross_start(0)
+        send_down(0, n_m)
         keep(0, inverse)
         keep(1, mf)
         cf = gathered(CF)
@@ -477,7 +475,6 @@
             if block in PIECES:
                 join(block)
             seen_copy(block, 0).start()
-        send_down(0, n_m)
         send_down(1, n_c)
 
         inverse = negated_inverse(a_ref, in_ref[6] + unpack(crossed(0)))
@@ -488,8 +485,6 @@
         keep(3, inverse)
         keep(4, cm)
         send_all(3, q_c)
-        down_copy(2, 0, outer).wait_recv()
-        after_fine()
 
     @pl.when(is_other)
     def _():
@@ -500,6 +495,10 @@
                 seen_copy(block, slot_here + 1).start()
             else:
                 gram_copy(block, slot_here).start()
+
+    @pl.when(has_outer)
+    def _():
+        pass_on(0)
 
     @pl.when(is_helper)
     def _():
@@ -514,9 +513,8 @@
         cross_start(4)
         send_answer(0, n_y)
 
-    @pl.when(is_other)
-    def _():
-        pass_on(0)
+    @pl.when(has_outer)
+    def _():
         pass_on(1)
 
     @pl.when(is_helper)
@@ -529,10 +527,16 @@
 
     @pl.when(is_other)
     def _():
-        down_copy(2, 0, outer).wait_recv()
-        after_fine()
         last_copy(0, 1).wait_recv()
         swap(0)
+
+    @pl.when(is_other & ((outer < 0) | (outer >= n_leaf)))
+    def _():
+        down_copy(0, 0, outer).wait_recv()
+        down_copy(1, 0, outer).wait_recv()
+
+    down_copy(2, 0, outer).wait_recv()
+    after_fine()
 
     def others_arrived(block):
         for step in range(1, n_top):

time: 28.4 us -> 28.2 us (level)
  Pallas kernels: 27.6 us -> 27.2 us
    pallas_call x1, Pallas kernels: 27.6 us -> 27.2 us  [local(): pl.pallas_call(functools.partial(kernel, n_leaf, n_mid, n_top), out_shape...]
where the time goes in v4:
time: 28.2 us; the launch traced here: 27.9 us
  Pallas kernels  27.2 us (96%)
  local copies, waits for them, and re-layouts  0.63 us (2%)
    pallas_call x1, Pallas kernels, local(): pl.pallas_call(functools.partial(kernel, n_leaf, n_mid, n_top), out_shape...  27.2 us
    unnamed x1, local copies, waits for them, and re-layouts  0.63 us

profile of v4, /device:TPU:0, one launch (start us, length us, event | category | flops | bytes accessed | tf_op | source)
XLA Modules:
  0.0 27.9 jit_solution(6313937308525807346)
XLA Ops:
  0.0 27.2 %shard_map.82 = f32[128,128]{1,0:T(8,128)S(1)} custom-call(f32[128,128]{1,0:T(8,128)} %bitcast.7, f32[128,128]{1,0:T(8,128)} %bitcast.8, f32[128,128]{1,0:T(8,128)} %bitcast.9, f32[128,128]{1,0:T(8,128)} %bitcast.10, f32[128,128]{1,0:T(8,128)} %core_fine_hbm.1, f32[128,128]{1,0:T(8,128)} %core_mid_hbm.1, f32[128,128]{1,0:T(8,128)} %core_coarse_hbm.1, ...), custom_call_target="tpu_custom_call" | custom-call | tf_op jit(solution)/shard_map/pallas_call | solution.py:623
  27.2 0.6 %copy.10 = f32[1,1,1,128,128]{4,3,2,1,0:T(8,128)} copy(f32[1,1,1,128,128]{4,3,2,1,0:T(8,128)S(1)} %bitcast.6) | data formatting | bytes 131072

commit v5 on v4

--- a/solution.py
+++ b/solution.py
@@ -471,11 +471,11 @@
         cross_start(1)
         store(cross_ref, 3, corrected(CC, lost[:, r:]), True)
         cross_start(3)
+        send_down(1, n_c)
         for block in SEEN:
             if block in PIECES:
                 join(block)
             seen_copy(block, 0).start()
-        send_down(1, n_c)
 
         inverse = negated_inverse(a_ref, in_ref[6] + unpack(crossed(0)))
         cm = crossed(1)
@@ -505,13 +505,13 @@
         for number in range(2):
             help_copy(number).wait_recv()
         n_y = dot(seen(YF), kept_ref[0])
+        send_answer(0, n_y)
         help_copy(2).wait_recv()
         lost = dot_nt(n_y, kept_ref[1:3].reshape(2 * r, r))
         cross_ref[2] = corrected(YM, lost[:, :r])
         cross_start(2)
         cross_ref[4] = corrected(YC, lost[:, r:])
         cross_start(4)
-        send_answer(0, n_y)
 
     @pl.when(has_outer)
     def _():

time: 28.2 us -> 27.9 us (0.989)
  Pallas kernels: 27.2 us -> 26.9 us
    pallas_call x1, Pallas kernels: 27.2 us -> 26.9 us  [local(): pl.pallas_call(functools.partial(kernel, n_leaf, n_mid, n_top), out_shape...]
where the time goes in v5:
time: 27.9 us; the launch traced here: 27.6 us
  Pallas kernels  26.9 us (96%)
  local copies, waits for them, and re-layouts  0.63 us (2%)
    pallas_call x1, Pallas kernels, local(): pl.pallas_call(functools.partial(kernel, n_leaf, n_mid, n_top), out_shape...  26.9 us
    unnamed x1, local copies, waits for them, and re-layouts  0.63 us

profile of v5, /device:TPU:0, one launch (start us, length us, event | category | flops | bytes accessed | tf_op | source)
XLA Modules:
  0.0 27.6 jit_solution(12702846875286723014)
XLA Ops:
  0.0 26.9 %shard_map.82 = f32[128,128]{1,0:T(8,128)S(1)} custom-call(f32[128,128]{1,0:T(8,128)} %bitcast.7, f32[128,128]{1,0:T(8,128)} %bitcast.8, f32[128,128]{1,0:T(8,128)} %bitcast.9, f32[128,128]{1,0:T(8,128)} %bitcast.10, f32[128,128]{1,0:T(8,128)} %core_fine_hbm.1, f32[128,128]{1,0:T(8,128)} %core_mid_hbm.1, f32[128,128]{1,0:T(8,128)} %core_coarse_hbm.1, ...), custom_call_target="tpu_custom_call" | custom-call | tf_op jit(solution)/shard_map/pallas_call | solution.py:623
  27.0 0.6 %copy.10 = f32[1,1,1,128,128]{4,3,2,1,0:T(8,128)} copy(f32[1,1,1,128,128]{4,3,2,1,0:T(8,128)S(1)} %bitcast.6) | data formatting | bytes 131072

commit v6 on v5

--- a/solution.py
+++ b/solution.py
@@ -532,10 +532,10 @@
 
     @pl.when(is_other & ((outer < 0) | (outer >= n_leaf)))
     def _():
-        down_copy(0, 0, outer).wait_recv()
-        down_copy(1, 0, outer).wait_recv()
-
-    down_copy(2, 0, outer).wait_recv()
+        down_copy(0, 0, root).wait_recv()
+        down_copy(1, 0, root).wait_recv()
+
+    down_copy(2, 0, root).wait_recv()
     after_fine()
 
     def others_arrived(block):

time: 27.9 us -> 27.9 us (level)
  no operation moved by 1% of the time
where the time goes in v6:
time: 27.9 us; the launch traced here: 27.6 us
  Pallas kernels  26.9 us (96%)
  local copies, waits for them, and re-layouts  0.63 us (2%)
    pallas_call x1, Pallas kernels, local(): pl.pallas_call(functools.partial(kernel, n_leaf, n_mid, n_top), out_shape...  26.9 us
    unnamed x1, local copies, waits for them, and re-layouts  0.63 us

profile of v6, /device:TPU:0, one launch (start us, length us, event | category | flops | bytes accessed | tf_op | source)
XLA Modules:
  0.0 27.6 jit_solution(12702846875286723014)
XLA Ops:
  0.0 26.9 %shard_map.82 = f32[128,128]{1,0:T(8,128)S(1)} custom-call(f32[128,128]{1,0:T(8,128)} %bitcast.7, f32[128,128]{1,0:T(8,128)} %bitcast.8, f32[128,128]{1,0:T(8,128)} %bitcast.9, f32[128,128]{1,0:T(8,128)} %bitcast.10, f32[128,128]{1,0:T(8,128)} %core_fine_hbm.1, f32[128,128]{1,0:T(8,128)} %core_mid_hbm.1, f32[128,128]{1,0:T(8,128)} %core_coarse_hbm.1, ...), custom_call_target="tpu_custom_call" | custom-call | tf_op jit(solution)/shard_map/pallas_call | solution.py:623
  27.0 0.6 %copy.10 = f32[1,1,1,128,128]{4,3,2,1,0:T(8,128)} copy(f32[1,1,1,128,128]{4,3,2,1,0:T(8,128)S(1)} %bitcast.6) | data formatting | bytes 131072

commit v7 on v6

--- a/solution.py
+++ b/solution.py
@@ -456,13 +456,13 @@
     @pl.when(is_root)
     def _():
         inverse = negated_inverse(a_ref, in_ref[5] + unpack(gathered(FF)))
+        keep(0, inverse)
         mf = gathered(MF)
+        keep(1, mf)
         n_m = dot(mf, inverse)
         store(cross_ref, 0, unpack(gathered(MM)) + dot_nt(n_m, mf), True)
         cross_start(0)
         send_down(0, n_m)
-        keep(0, inverse)
-        keep(1, mf)
         cf = gathered(CF)
         n_c = dot(cf, inverse)
         keep(2, cf)
@@ -478,12 +478,12 @@
             seen_copy(block, 0).start()
 
         inverse = negated_inverse(a_ref, in_ref[6] + unpack(crossed(0)))
+        keep(3, inverse)
         cm = crossed(1)
+        keep(4, cm)
         q_c = dot(cm, inverse)
         store(last_ref.at[top], 0, unpack(crossed(3)) + dot_nt(q_c, cm), True)
         send_last(0)
-        keep(3, inverse)
-        keep(4, cm)
         send_all(3, q_c)
 
     @pl.when(is_other)

time: 27.9 us -> 28 us (level)
  no operation moved by 1% of the time
where the time goes in v7:
time: 28 us; the launch traced here: 27.7 us
  Pallas kernels  27 us (96%)
  local copies, waits for them, and re-layouts  0.63 us (2%)
    pallas_call x1, Pallas kernels, local(): pl.pallas_call(functools.partial(kernel, n_leaf, n_mid, n_top), out_shape...  27 us
    unnamed x1, local copies, waits for them, and re-layouts  0.63 us

profile of v7, /device:TPU:0, one launch (start us, length us, event | category | flops | bytes accessed | tf_op | source)
XLA Modules:
  0.0 27.7 jit_solution(18426414893051903222)
XLA Ops:
  0.0 27.0 %shard_map.82 = f32[128,128]{1,0:T(8,128)S(1)} custom-call(f32[128,128]{1,0:T(8,128)} %bitcast.7, f32[128,128]{1,0:T(8,128)} %bitcast.8, f32[128,128]{1,0:T(8,128)} %bitcast.9, f32[128,128]{1,0:T(8,128)} %bitcast.10, f32[128,128]{1,0:T(8,128)} %core_fine_hbm.1, f32[128,128]{1,0:T(8,128)} %core_mid_hbm.1, f32[128,128]{1,0:T(8,128)} %core_coarse_hbm.1, ...), custom_call_target="tpu_custom_call" | custom-call | tf_op jit(solution)/shard_map/pallas_call | solution.py:623
  27.0 0.6 %copy.10 = f32[1,1,1,128,128]{4,3,2,1,0:T(8,128)} copy(f32[1,1,1,128,128]{4,3,2,1,0:T(8,128)S(1)} %bitcast.6) | data formatting | bytes 131072
